TPU v7x, 32 devices: a whole 2x2x4 slice. The times are simulated.
32 devices in a mesh: seq: 8 (over z, x), head: 4 (over y, core).
Axes of the slice: x: 2, y: 2, z: 4, core: 2. Of those that a mesh axis runs over, the one named last changes fastest.
Arguments:
- x_in: bfloat16 [8192, 4096], P('seq', 'head'), may hold values from -6 to 6
- z_gate: bfloat16 [8192, 4096], P('seq', 'head'), may hold values from -6 to 6
- b_in: bfloat16 [8192, 128], P('seq', 'head'), may hold values from -2 to 2
- c_in: bfloat16 [8192, 128], P('seq', 'head'), may hold values from -2 to 2
- dt_raw: float32 [8192, 64], P('seq', 'head'), may hold values from -4 to 4
- decay_rate: float32 [64], P('head'), may hold values from 6.1035156e-05 to 0.05, as said below
- skip_gain: float32 [64], P('head'), may hold values from 0.5 to 1.5
- norm_gain: float32 [4096], P('head'), may hold values from 0.1 to 1.9
- w_out: bfloat16 [4096, 2560], P('head'), may hold values from -0.09375 to 0.09375
- doc_lengths: int32 [32], replicated, may hold values from 1 to 2048, 8192 in all
Outputs:
- mixed: bfloat16 [8192, 2560], P(('seq', 'head'))
Inputs may be any that keep to these rules, and one draw needn't show every extreme that they name: `decay_rate`: every head's rate lies in the range. `doc_lengths`: they sum to 8192; the longest is exactly 2048.
All inputs are finite; a program needn't handle non-finite values.
Results may differ from a plain program's by a relative error of at most 0.018.
Values may be sent and summed in bfloat16 or wider, within the bound.
A program may use at most 128 MiB of HBM per device.

v0:
```python
import jax
import jax.numpy as jnp
from jax import lax
from jax.sharding import PartitionSpec as P

SPAN = 256


norm_eps = 1e-05


def entering(x, axis, combine, identity):
    length, place = (lax.axis_size(axis), lax.axis_index(axis))
    everything = jax.tree.map(
        lambda part, kind: lax.all_gather(part.astype(kind), axis), x, (jnp.bfloat16, jnp.bfloat16)
    )
    start = jax.tree.map(
        lambda part, zero: jnp.broadcast_to(jnp.asarray(zero, part.dtype), part.shape), x, identity
    )

    def lap(k, before):
        reached = k < place
        new = combine(
            before, jax.tree.map(lambda part, own: part[k].astype(own.dtype), everything, x)
        )
        return jax.tree.map(lambda a, b: jnp.where(reached, a, b), new, before)

    return lax.fori_loop(0, length, lap, start)


def on_device(
    x_in, z_gate, b_in, c_in, dt_raw, decay_rate, skip_gain, norm_gain, w_out, doc_lengths
):
    rows_here, local_width = x_in.shape
    local_heads = dt_raw.shape[1]
    head_size = local_width // local_heads
    head_groups = lax.axis_size("head")
    b_full, c_full = (
        lax.all_gather(b_in, "head", axis=1, tiled=True),
        lax.all_gather(c_in, "head", axis=1, tiled=True),
    )
    state_size = b_full.shape[1]
    spans = rows_here // SPAN
    offset = lax.axis_index("seq") * rows_here
    positions = offset + jnp.arange(rows_here, dtype=jnp.int32)
    doc_ends = jnp.cumsum(doc_lengths)
    doc_starts = doc_ends - doc_lengths
    doc_ids = jnp.sum((positions[:, None] >= doc_ends[None, :]).astype(jnp.int32), axis=1)
    start_flags = jnp.any(positions[:, None] == doc_starts[None, :], axis=1).astype(jnp.int32)
    step_size = jax.nn.softplus(dt_raw)
    log_decay = -step_size * decay_rate[None, :]
    inputs = x_in.reshape(spans, SPAN, local_heads, head_size)
    b_blocks = b_full.reshape(spans, SPAN, state_size)
    c_blocks = c_full.reshape(spans, SPAN, state_size)
    step_blocks = step_size.reshape(spans, SPAN, local_heads)
    decay_blocks = log_decay.reshape(spans, SPAN, local_heads)
    id_blocks = doc_ids.reshape(spans, SPAN)
    flag_blocks = start_flags.reshape(spans, SPAN)
    cumulative = jnp.cumsum(decay_blocks, axis=1)
    unreset = (jnp.cumsum(flag_blocks, axis=1) == 0).astype(jnp.float32)
    from_start = jnp.exp(cumulative) * unreset[:, :, None]

    def combine(earlier, latter):
        return (earlier[0] * latter[0], latter[1] + latter[0][:, None, None] * earlier[1])

    local_pos = jnp.arange(SPAN, dtype=jnp.int32)
    causal_mask = local_pos[:, None] >= local_pos[None, :]
    scores = jnp.einsum("cin,cjn->cij", c_blocks, b_blocks, preferred_element_type=jnp.float32)
    same_doc = causal_mask[None] & (id_blocks[:, :, None] == id_blocks[:, None, :])
    cum_heads = jnp.swapaxes(cumulative, 1, 2)
    differ = cum_heads[:, :, :, None] - cum_heads[:, :, None, :]
    decay_table = jnp.exp(jnp.where(same_doc[:, None], differ, -jnp.inf))
    weights = (
        scores[:, None] * decay_table * jnp.swapaxes(step_blocks, 1, 2)[:, :, None, :]
    ).astype(jnp.bfloat16)
    y_local = jnp.einsum("chij,cjhp->cihp", weights, inputs, preferred_element_type=jnp.float32)
    to_end = jnp.exp(cumulative[:, -1:, :] - cumulative) * (id_blocks == id_blocks[:, -1:])[
        :, :, None
    ].astype(jnp.float32)
    scaled = (inputs * (to_end * step_blocks)[:, :, :, None]).astype(jnp.bfloat16)
    block_states = jnp.einsum(
        "cjhp,cjn->chpn", scaled, b_blocks, preferred_element_type=jnp.float32
    )
    running = jnp.zeros((local_heads, head_size, state_size), jnp.float32)
    decay_total = jnp.ones((local_heads,), jnp.float32)
    befores = []
    for span_index in range(spans):
        befores.append(running)
        running = from_start[span_index, -1][:, None, None] * running + block_states[span_index]
        decay_total = decay_total * from_start[span_index, -1]
    scanned = entering(
        (decay_total, running),
        "seq",
        combine,
        (jnp.ones_like(decay_total), jnp.zeros_like(running)),
    )
    befores, incoming = (jnp.stack(befores), scanned[1])
    y_inter = (
        jnp.einsum(
            "cin,chpn->cihp", c_blocks.astype(jnp.float32), befores, precision=lax.Precision.HIGHEST
        )
        * from_start[:, :, :, None]
    )
    cum_device = jnp.cumsum(log_decay, axis=0)
    unreset_device = (jnp.cumsum(start_flags) == 0).astype(jnp.float32)
    from_device = jnp.exp(cum_device) * unreset_device[:, None]
    y_carry = (
        jnp.einsum(
            "tn,hpn->thp", c_full.astype(jnp.float32), incoming, precision=lax.Precision.HIGHEST
        )
        * from_device[:, :, None]
    )
    y_total = (y_local + y_inter).reshape(rows_here, local_heads, head_size) + y_carry
    y_total = y_total + skip_gain[None, :, None] * x_in.reshape(
        rows_here, local_heads, head_size
    ).astype(jnp.float32)
    gated = y_total.reshape(rows_here, local_width) * jax.nn.silu(z_gate.astype(jnp.float32))
    square_sums = jnp.sum(gated * gated, axis=1)
    normed = (gated * norm_gain[None, :]).astype(jnp.bfloat16)
    own_rows = rows_here // head_groups
    full_width = local_width * head_groups
    all_squares = lax.psum(square_sums, "head")
    row_squares = lax.dynamic_slice_in_dim(
        all_squares, lax.axis_index("head") * own_rows, own_rows, 0
    )
    summed = lax.psum_scatter(
        jnp.dot(normed, w_out, preferred_element_type=jnp.float32).astype(jnp.bfloat16),
        "head",
        scatter_dimension=0,
        tiled=True,
    ).astype(jnp.float32)
    inverse_rms = lax.rsqrt(row_squares / full_width + norm_eps)
    return (summed * inverse_rms[:, None]).astype(jnp.bfloat16)


def solution(mesh):
    return jax.shard_map(
        on_device,
        mesh=mesh,
        in_specs=(
            P("seq", "head"),
            P("seq", "head"),
            P("seq", "head"),
            P("seq", "head"),
            P("seq", "head"),
            P("head"),
            P("head"),
            P("head"),
            P("head", None),
            P(),
        ),
        out_specs=P(("seq", "head"), None),
        check_vma=False,
    )
```

profile of v0, /device:TPU:10, one launch (start us, length us, event | category | flops | bytes accessed | tf_op | source)
XLA Modules:
  0.0 180.0 jit_solution(10115949785182696612)
XLA Ops:
  6.5 0.7 copy.98
  7.4 0.7 sub.29
  8.6 1.2 reduce-window.41
  10.2 0.9 negate_multiply_fusion
  11.1 2.3 %reduce-window.39 = f32[4,16,2,128]{3,1,2,0:T(8,128)S(1)} reduce-window(f32[4,16,2,128]{3,1,2,0:T(8,128)S(1)} %copy_bitcast_fusion.1, f32[]{:T(128)} %constant.64.clone.1), window={size=1x1x1x128 pad=0_0x0_0x0_0x127_0}, to_apply=%region_2.3 | reduce-window | flops 2080768 | bytes 131076 | tf_op jit(solution)/shard_map/reduce-window.1
  13.6 0.7 copy_bitcast_fusion
  14.9 6.0 %all_gather.15 = bf16[1024,128]{0,1:T(8,128)(2,1)S(1)} all-gather(bf16[1024,32]{0,1:T(8,128)(2,1)} %param.14), channel_id=1, replica_groups=mesh['seq'=8,'head'=4] {'head'}, dimensions={1}, use_global_device_ids=true | all-gather | bytes 327680 | tf_op jit(solution)/shard_map/all_gather | solution.py:39
  21.1 4.0 %copy.105 = bf16[1024,1024]{0,1:T(8,128)(2,1)} copy(bf16[1024,1024]{1,0:T(8,128)(2,1)} %param.12) | data formatting | bytes 4194304 | tf_op args[0]
  25.0 3.3 %reshape.270 = bf16[4,256,16,64]{1,0,3,2:T(4,128)(2,1)S(1)} reshape(bf16[1024,1024]{0,1:T(8,128)(2,1)} %copy.105) | data formatting | bytes 4194304 | tf_op jit(solution)/shard_map/reshape | solution.py:52
  28.4 1.0 multiply_convert_fusion.3
  29.4 0.3 copy-done.1
  29.7 0.7 fusion.23
  30.4 1.4 fusion.28
  32.0 3.0 %copy.116 = f32[1024,1024]{0,1:T(8,128)} copy(bf16[1024,1024]{1,0:T(8,128)(2,1)S(1)} %copy-done) | data formatting | bytes 6291456 | tf_op jit(solution)/shard_map/convert_element_type | solution.py:116
  35.4 0.6 reduce-window.57
  36.0 4.5 %reduce-window.54 = f32[16,8,128]{2,1,0:T(8,128)S(1)} reduce-window(f32[16,8,128]{2,1,0:T(8,128)S(1)} %bitcast.124, f32[]{:T(128)} %constant.64.clone.1), window={size=1x1x128 pad=0_0x0_0x127_0}, to_apply=%region_9.10 | reduce-window | flops 2080768 | bytes 131076 | tf_op jit(solution)/shard_map/reduce-window.5
  40.8 0.6 copy.104
  41.6 14.5 %all-gather = bf16[8,1,16]{2,1,0:T(2,128)(2,1)S(1)} all-gather(bf16[1,1,16]{2,1,0:T(2,128)(2,1)S(1)} %copy.113), channel_id=2, replica_groups=mesh['seq'=8,'head'=4] {'seq'}, dimensions={0}, use_global_device_ids=true | all-gather | bytes 288 | tf_op jit(solution)/shard_map/all_gather | solution.py:15
  56.1 0.6 copy.148
  56.7 5.9 %all_gather.14 = bf16[1024,128]{0,1:T(8,128)(2,1)S(1)} all-gather(bf16[1024,32]{0,1:T(8,128)(2,1)S(1)} %copy-done.4), channel_id=1, replica_groups=mesh['seq'=8,'head'=4] {'head'}, dimensions={1}, use_global_device_ids=true | all-gather | bytes 327680 | tf_op jit(solution)/shard_map/all_gather | solution.py:40
  63.4 3.2 %fusion.16 = f32[4,16,64,256]{3,2,1,0:T(8,128)S(1)} fusion(bf16[4,256,128,1]{2,1,3,0:T(8,128)(2,1)S(1)} %bitcast.118, f32[1,16,64,128]{3,2,1,0:T(8,128)} %get-tuple-element.133, f32[1,16,64,128]{3,2,1,0:T(8,128)} %get-tuple-element.134, f32[1,16,64,128]{3,2,1,0:T(8,128)} %get-tuple-element.135, f32[4]{0:T(128)S(1)} %pad.clone), kind=kOutput, calls=%fused_computation.28 | convolution fusion | flops 1612185600 | bytes 6029328 | tf_op jit(solution)/shard_map/cin,chpn->cihp/dot_general | solution.py:99
  66.7 5.3 %fusion.15 = f32[4,16,8,8,256]{4,3,2,1,0:T(8,128)S(1)} fusion(f32[4,16,64,256]{3,2,1,0:T(8,128)S(1)} %fusion.16, f32[4,16,256]{2,1,0:T(8,128)S(1)} %copy-done.6, f32[4,16,256]{2,1,0:T(8,128)S(1)} %copy-done.5, f32[4,256,256]{2,1,0:T(8,128)S(1)} %fusion.38, pred[4,256,256]{2,1,0:T(8,128)(4,1)S(1)} %compare_and_fusion, ...), kind=kOutput, calls=%fused_computation.23 | convolution fusion | flops 559939584 | bytes 11993088 | tf_op jit(solution)/shard_map/chij,cjhp->cihp/dot_general | solution.py:76
  72.0 2.7 %copy.125 = f32[4,16,8,8,256]{4,3,0,2,1:T(8,128)} copy(f32[4,16,8,8,256]{4,3,2,1,0:T(8,128)S(1)} %fusion.15) | data formatting | bytes 8388608 | tf_op jit(solution)/shard_map/reshape | solution.py:113
  74.9 6.5 %all-gather.3.cloned.1.call-done = bf16[8,16,64,128]{3,2,1,0:T(8,128)(2,1)} async-done(((bf16[1,16,64,128]{3,2,1,0:T(8,128)(2,1)}), bf16[8,16,64,128]{3,2,1,0:T(8,128)(2,1)}) %all-gather.3.cloned.1.call-update) | async-done | bytes 2097168 | tf_op jit(solution)/shard_map/all_gather | solution.py:15
  81.4 14.3 %while.14 = (s32[]{:T(128)}, f32[16,64,128]{2,1,0:T(8,128)S(1)}, s32[]{:T(128)}, bf16[8,16,64,128]{3,2,1,0:T(8,128)(2,1)}, bf16[8,16]{1,0:T(8,128)(2,1)}, /*index=5*/s32[]{:T(128)}, s32[]{:T(128)}) while((s32[]{:T(128)}, f32[16,64,128]{2,1,0:T(8,128)S(1)}, s32[]{:T(128)}, bf16[8,16,64,128]{3,2,1,0:T(8,128)(2,1)}, ...), condition=%wide.region_8.9_spmd.clone, body=%wide.region_7.8_spmd.clone.sunk | while | flops 655380 | bytes 1310993 | solution.py:28
  81.4 0.7 bitcast_convert_fusion.2
  82.1 1.1 fusion.46
  83.2 0.7 bitcast_convert_fusion.2
  83.9 1.1 fusion.46
  85.0 0.7 bitcast_convert_fusion.2
  85.7 1.1 fusion.46
  86.8 0.7 bitcast_convert_fusion.2
  87.5 1.1 fusion.46
  88.6 0.7 bitcast_convert_fusion.2
  89.2 1.1 fusion.46
  90.4 0.7 bitcast_convert_fusion.2
  91.0 1.1 fusion.46
  92.1 0.7 bitcast_convert_fusion.2
  92.8 1.1 fusion.46
  93.9 0.7 bitcast_convert_fusion.2
  94.6 1.1 fusion.46
  95.7 7.7 %fusion.13 = f32[1024,16,64]{0,2,1:T(8,128)} fusion(f32[1024,16,64]{0,2,1:T(8,128)} %bitcast.113, f32[1024,16,64]{0,2,1:T(8,128)} %bitcast.112, f32[16,64,128]{2,1,0:T(8,128)S(1)} %get-tuple-element.99, f32[16]{0:T(128)S(1)} %copy-done.8, f32[1024,16]{0,1:T(8,128)S(1)} %fusion.30, bf16[1024,128]{0,1:T(8,128)(2,1)S(1)} %all_gather.14), kind=kOutput, calls=%fused_computation.20 | convolution fusion | flops 1614807040 | bytes 13434944 | tf_op jit(solution)/shard_map/tn,hpn->thp/dot_general | solution.py:108
  103.4 5.5 %copy.117 = f32[1024,1024]{1,0:T(8,128)} copy(f32[1024,1024]{0,1:T(8,128)} %bitcast.114) | data formatting | bytes 8388608 | tf_op jit(solution)/shard_map/reshape | solution.py:117
  108.9 10.7 %convolution_convert_fusion = bf16[1024,2560]{1,0:T(8,128)(2,1)} fusion(bf16[1024,2560]{1,0:T(8,128)(2,1)} %param.20, f32[1024]{0:T(1024)S(1)} %copy-done.9, f32[1024,1024]{1,0:T(8,128)} %copy.117, bf16[1024,1024]{1,0:T(8,128)(2,1)S(1)} %copy-done.3), kind=kOutput, calls=%fused_computation.11 | convolution fusion | flops 5379719168 | bytes 16781312 | tf_op jit(solution)/shard_map/dot_general | solution.py:127
  119.7 3.5 %multiply_reduce_fusion = f32[1024]{0:T(1024)S(1)} fusion(f32[1024,1024]{1,0:T(8,128)} %copy.117, bf16[1024,1024]{1,0:T(8,128)(2,1)S(1)} %copy-done.3), kind=kLoop, calls=%fused_computation.24 | loop fusion | flops 8387584 | bytes 6295552 | tf_op jit(solution)/shard_map/reduce_sum | solution.py:118
  123.2 5.7 %psum.7 = f32[1024]{0:T(1024)S(1)} all-reduce(f32[1024]{0:T(1024)S(1)} %multiply_reduce_fusion), channel_id=1, replica_groups=mesh['seq'=8,'head'=4] {'head'}, use_global_device_ids=true, to_apply=%region_15.16 | all-reduce | flops 1024 | bytes 8192 | tf_op jit(solution)/shard_map/psum | solution.py:122
  128.9 41.6 %reduce-scatter.2.cloned.1.call-done = bf16[256,2560]{1,0:T(8,128)(2,1)} async-done(((bf16[1024,2560]{1,0:T(8,128)(2,1)}), bf16[256,2560]{1,0:T(8,128)(2,1)}) %reduce-scatter.2.cloned.1.call-update) | async-done | bytes 1310736 | tf_op jit(solution)/shard_map/reduce_scatter | solution.py:126
  170.6 2.7 %multiply_convert_fusion.4 = bf16[256,2560]{1,0:T(8,128)(2,1)} fusion(bf16[256,2560]{1,0:T(8,128)(2,1)} %reduce-scatter.2.cloned.1.call-done, f32[256]{0:T(256)S(1)} %add_rsqrt_fusion), kind=kLoop, calls=%fused_computation.27 | loop fusion | flops 1966080 | bytes 2622464 | tf_op jit(solution)/shard_map/convert_element_type | solution.py:133
  (72 shorter events, 4.1 us)
Async XLA Ops:
  6.5 74.9 %all-gather.3.cloned.1.call-start = ((), (), s32[]{:S(2)}) async-start(), calls=%async_computation.1 | async-start | bytes 2359296 | tf_op jit(solution)/shard_map/all_gather | solution.py:15
  28.4 1.3 copy-start.1
  29.7 2.2 %copy-start = (bf16[1024,1024]{1,0:T(8,128)(2,1)S(1)}, bf16[1024,1024]{1,0:T(8,128)(2,1)}, u32[]{:S(2)}) copy-start(bf16[1024,1024]{1,0:T(8,128)(2,1)} %param.12) | copy-start | bytes 6291460
  31.8 24.9 %copy-start.4 = (bf16[1024,32]{0,1:T(8,128)(2,1)S(1)}, bf16[1024,32]{0,1:T(8,128)(2,1)}, u32[]{:S(2)}) copy-start(bf16[1024,32]{0,1:T(8,128)(2,1)} %param.15) | copy-start | bytes 196612
  31.9 138.7 %reduce-scatter.2.cloned.1.call-start = ((), (), s32[]{:S(2)}) async-start(), calls=%async_computation.2 | async-start | bytes 6553600 | tf_op jit(solution)/shard_map/reduce_scatter | solution.py:126
  62.6 4.0 %copy-start.2 = (bf16[4,256,16,64]{1,0,3,2:T(4,128)(2,1)S(1)}, bf16[4,256,16,64]{1,0,3,2:T(4,128)(2,1)}, u32[]{:S(2)}) copy-start(bf16[4,256,16,64]{1,0,3,2:T(4,128)(2,1)} %copy-done.1) | copy-start | bytes 6291460
  62.8 3.8 %copy-start.5 = (f32[4,16,256]{2,1,0:T(8,128)S(1)}, f32[4,16,256]{2,1,0:T(8,128)}, u32[]{:S(2)}) copy-start(f32[4,16,256]{2,1,0:T(8,128)} %get-tuple-element.136) | copy-start | bytes 196612
  62.8 3.8 %copy-start.6 = (f32[4,16,256]{2,1,0:T(8,128)S(1)}, f32[4,16,256]{2,1,0:T(8,128)}, u32[]{:S(2)}) copy-start(f32[4,16,256]{2,1,0:T(8,128)} %copy.104) | copy-start | bytes 196612
  71.9 2.7 %copy-start.7 = (s32[9,1]{1,0:T(8,128)S(1)}, s32[9,1]{1,0:T(8,128)}, u32[]{:S(2)}) copy-start(s32[9,1]{1,0:T(8,128)} %reduce-window.57) | copy-start | bytes 112
  74.6 21.1 %copy-start.8 = (f32[16]{0:T(128)S(1)}, f32[16]{0:T(128)}, u32[]{:S(2)}) copy-start(f32[16]{0:T(128)} %param.18) | copy-start | bytes 196
  103.4 5.5 %copy-start.3 = (bf16[1024,1024]{1,0:T(8,128)(2,1)S(1)}, bf16[1024,1024]{1,0:T(8,128)(2,1)}, u32[]{:S(2)}) copy-start(bf16[1024,1024]{1,0:T(8,128)(2,1)} %param.13) | copy-start | bytes 6291460
  103.4 5.5 %copy-start.9 = (f32[1024]{0:T(1024)S(1)}, f32[1024]{0:T(1024)}, u32[]{:S(2)}) copy-start(f32[1024]{0:T(1024)} %param.19) | copy-start | bytes 12292
Sparse Core Ops, SparseCore 0:
  32.0 49.3 all-gather.2
  119.8 50.7 reduce-scatter.1
where the time goes:
time: 183 us; the launch traced here: 180 us
  waiting for transfers between devices  48.1 us (26%)
  other arithmetic  35.5 us (19%)
  blocking collectives  32.1 us (18%)
  matrix products  27.9 us (15%)
  local copies, waits for them, and re-layouts  22.6 us (12%)
  between operations  13.7 us (7%)
    reduce_scatter x1, waiting for transfers between devices, on_device(): lax.psum_scatter(jnp.dot(normed, w_out, preferred_element_type=jnp.float3...  41.6 us
    all_gather x1, blocking collectives, entering(): lax.all_gather(part.astype(kind), axis)  14.5 us
    dot_general x1, matrix products, on_device(): jnp.dot(normed, w_out, preferred_element_type=jnp.float32)  10.7 us
    another operation x11, other arithmetic  9.88 us
    select_n x8, other arithmetic, lap(): return jax.tree.map(lambda a, b: jnp.where(reached, a, b), new, before)  8.7 us
    dot_general x1, matrix products, on_device(): jnp.einsum('tn,hpn->thp', c_full.astype(jnp.float32), incoming, precision...  7.7 us
    all_gather x1, waiting for transfers between devices, entering(): lax.all_gather(part.astype(kind), axis)  6.47 us
    all_gather x1, blocking collectives, on_device(): lax.all_gather(b_in, 'head', axis=1, tiled=True)  5.99 us
  transfers between devices with their start and end apart: 2, of which 2 were waited for; matrix products, arithmetic and copies ran while one was open for 14% of the time, Pallas kernels for 0%

commit v1 on v0

v1 whole, which is shorter than its diff:
```python
import functools

import jax
import jax.numpy as jnp
from jax import lax
from jax.experimental import pallas as pl
from jax.experimental.pallas import tpu as pltpu
from jax.sharding import PartitionSpec as P

norm_eps = 1e-05
MESH = pl.DeviceIdType.MESH
F32, BF16 = jnp.float32, jnp.bfloat16


def halves(v):
    high = v.astype(BF16).astype(F32)
    return high, v - high


def kernel(
    dims,
    bc_ref,
    dt_ref,
    rate_ref,
    skip_ref,
    gain_ref,
    ends_ref,
    x_hbm,
    z_hbm,
    w_hbm,
    out_ref,
    x_v,
    z_v,
    w_v,
    bc_all,
    xf_v,
    at_v,
    g_v,
    dec_v,
    cal_v,
    y_v,
    eg_v,
    st_send,
    st_recv,
    gin_v,
    nrm_v,
    own_v,
    a_send,
    a_recv,
    b_send,
    b_recv,
    sq_send,
    sq_recv,
    loc_sem,
    bc_ssem,
    bc_rsem,
    st_ssem,
    st_rsem,
    sq_ssem,
    sq_rsem,
    a_ssem,
    a_rsem,
    b_ssem,
    b_rsem,
):
    n_seq, groups, blk, heads, reach, chunks = dims
    rows, width = x_v.shape
    part = bc_ref.shape[0] // 2
    n_state = part * groups
    head_size = width // heads
    cw = w_v.shape[1] // chunks
    hd = lax.axis_index("head")
    sq = lax.axis_index("seq")
    p1 = hd + 1 - 2 * (hd % 2)
    p2 = (hd + 2) % 4
    p3 = (p1 + 2) % 4
    rel = (hd, p1, p2, p3)

    loads = [
        pltpu.make_async_copy(src, dst, loc_sem.at[i])
        for i, (src, dst) in enumerate(
            ((x_hbm, x_v), (z_hbm, z_v), (w_hbm, w_v), (bc_ref, bc_all.at[hd]))
        )
    ]
    loads[0].start()
    loads[3].start()

    barrier = pltpu.get_barrier_semaphore()
    for k in (1, 2, 3):
        pl.semaphore_signal(
            barrier, inc=1, device_id={"seq": sq, "head": rel[k]}, device_id_type=MESH
        )
    for k in range(1, reach + 1):
        for other in ((sq + k) % n_seq, (sq + n_seq - k) % n_seq):
            pl.semaphore_signal(
                barrier, inc=1, device_id={"seq": other, "head": hd}, device_id_type=MESH
            )
    pl.semaphore_wait(barrier, 3 + 2 * reach)

    def to_head(k, src, dst, ssem, rsem):
        return pltpu.make_async_remote_copy(
            src_ref=src,
            dst_ref=dst,
            send_sem=ssem,
            recv_sem=rsem,
            device_id={"seq": sq, "head": rel[k]},
            device_id_type=MESH,
        )

    bc_copies = [
        to_head(k, bc_ref, bc_all.at[hd], bc_ssem.at[k], bc_rsem.at[k]) for k in (1, 2, 3)
    ]
    for copy in bc_copies:
        copy.start()
    loads[1].start()
    loads[2].start()

    step = jnp.log(1.0 + jnp.exp(dt_ref[...]))
    ld = -step * rate_ref[...]
    l1, rest = halves(ld)
    l2, l3 = halves(rest)
    split = jnp.concatenate([l1, l2, l3], axis=0).astype(BF16)
    ii = lax.broadcasted_iota(jnp.int32, (blk, blk), 0)
    jj = lax.broadcasted_iota(jnp.int32, (blk, blk), 1)
    upper = jnp.where(ii <= jj, 1.0, 0.0).astype(BF16)
    er = lax.broadcasted_iota(jnp.int32, (128, width), 0)
    ec = lax.broadcasted_iota(jnp.int32, (128, width), 1)
    lead = ec // head_size
    spread_f = jnp.where((er == lead) | (er == lead + heads), 1.0, 0.0).astype(BF16)
    spread_e = jnp.where(
        (er == lead + 2 * heads) | (er == lead + 3 * heads), 1.0, 0.0
    ).astype(BF16)
    pad = jnp.zeros((128 - 4 * heads, blk), F32)
    lasts = []
    for s in range(groups):
        at = slice(s * blk, (s + 1) * blk)
        c3 = jnp.dot(split[:, at], upper, preferred_element_type=F32)
        cum = c3[:heads] + c3[heads : 2 * heads] + c3[2 * heads :]
        fh, fl = halves(jnp.exp(-cum) * step[:, at])
        eh, el = halves(jnp.exp(cum))
        turned = jnp.concatenate([fh, fl, eh, el, pad], axis=0).T.astype(BF16)
        at_v[s] = turned
        lasts.append(
            jnp.dot(turned[blk - 16 :], spread_e, preferred_element_type=F32)[15:16]
        )
        if s == 0:
            loads[0].wait()
        fx = jnp.dot(turned, spread_f, preferred_element_type=F32)
        xf_v[s] = (x_v[at, :].astype(F32) * fx).astype(BF16)

    base = sq * rows
    pos = base + lax.broadcasted_iota(jnp.int32, (8, rows), 1)
    doc = jnp.zeros((8, rows), F32)
    marks = [base + s * blk - 1 for s in range(groups + 1)]
    tags = [jnp.float32(0.0)] * (groups + 1)
    for k in range(ends_ref.shape[0]):
        end = ends_ref[k]
        doc = doc + jnp.where(pos >= end, 1.0, 0.0)
        tags = [t + jnp.where(m >= end, 1.0, 0.0) for t, m in zip(tags, marks)]

    for copy in bc_copies:
        copy.wait_recv()
    loads[3].wait()
    bt = jnp.concatenate([bc_all[k, :part, :] for k in range(groups)], axis=0)
    ct = jnp.concatenate([bc_all[k, part:, :] for k in range(groups)], axis=0)

    state = jnp.zeros((n_state, width), F32)
    decay = jnp.ones((1, width), F32)
    for s in range(groups):
        at = slice(s * blk, (s + 1) * blk)
        g_v[s] = state.astype(BF16)
        dec_v[s] = jnp.broadcast_to(decay, (8, width))
        kept = jnp.where(doc[:1, at] == tags[s + 1], 1.0, 0.0)
        bm = (bt[:, at].astype(F32) * kept).astype(BF16)
        grown = jnp.dot(bm, xf_v[s], preferred_element_type=F32)
        alive = jnp.where(tags[s] == tags[s + 1], 1.0, 0.0)
        state = lasts[s] * (alive * state + grown)
        decay = decay * (lasts[s] * alive)
    st_send[:n_state, :] = state.astype(BF16)
    st_send[n_state:, :] = jnp.broadcast_to(decay, (16, width)).astype(BF16)

    def to_later(k):
        return pltpu.make_async_remote_copy(
            src_ref=st_send,
            dst_ref=st_recv.at[k - 1],
            send_sem=st_ssem.at[k - 1],
            recv_sem=st_rsem.at[k - 1],
            device_id={"seq": (sq + k) % n_seq, "head": hd},
            device_id_type=MESH,
        )

    for k in range(1, reach + 1):

        @pl.when(sq + k < n_seq)
        def _():
            to_later(k).start()

    loads[1].wait()
    for s in range(groups):
        at = slice(s * blk, (s + 1) * blk)
        c_s = ct[:, at].astype(F32).T
        scores = jnp.dot(c_s.astype(BF16), bt[:, at], preferred_element_type=F32)
        row = doc[:1, at]
        col = jnp.broadcast_to(row, (128, blk)).T[:, :1]
        seen = (ii >= jj) & (col == row)
        scores = jnp.where(seen, scores, 0.0).astype(BF16)
        cal = (c_s * jnp.where(col == tags[s], 1.0, 0.0)).astype(BF16)
        cal_v[s] = cal
        ex = jnp.dot(at_v[s], spread_e, preferred_element_type=F32)
        y = jnp.dot(scores, xf_v[s], preferred_element_type=F32)
        y = y + jnp.dot(cal, g_v[s], preferred_element_type=F32)
        zf = z_v[at, :].astype(F32)
        gate = zf / (1.0 + jnp.exp(-zf))
        y_v[s] = (ex * y + skip_ref[...] * x_v[at, :].astype(F32)) * gate
        eg_v[s] = ex * gate

    for k in range(1, reach + 1):

        @pl.when(sq >= k)
        def _():
            to_later(k).wait_recv()

        @pl.when(sq < k)
        def _():
            st_recv[k - 1] = jnp.zeros(st_recv.shape[1:], BF16)

    incoming = jnp.zeros((n_state, width), F32)
    for k in range(reach, 0, -1):
        incoming = (
            st_recv[k - 1, :n_state, :].astype(F32)
            + st_recv[k - 1, n_state : n_state + 1, :].astype(F32) * incoming
        )
    gin_v[...] = incoming

    def normed_of(q):
        carried = (gin_v[...] * dec_v[q][:1]).astype(BF16)
        u = y_v[q] + eg_v[q] * jnp.dot(cal_v[q], carried, preferred_element_type=F32)
        total = jnp.sum(u * u, axis=1, keepdims=True)
        nrm_v[...] = (u * gain_ref[...]).astype(BF16)
        return jnp.broadcast_to(total, (blk, 128)).T[:8]

    def product(c):
        return jnp.dot(nrm_v[...], w_v[:, c * cw : (c + 1) * cw], preferred_element_type=F32)

    def a_copy(t, c):
        i = t * chunks + c
        return to_head(1, a_send.at[i], a_recv.at[i], a_ssem.at[i], a_rsem.at[i])

    def b_copy(c):
        return to_head(2, b_send.at[c], b_recv.at[c], b_ssem.at[c], b_rsem.at[c])

    def sq_copy(k):
        return to_head(
            k, sq_send.at[k], sq_recv.at[k], sq_ssem.at[k], sq_rsem.at[k]
        )

    loads[2].wait()
    for t, k in ((0, 3), (None, 2), (1, 1), (None, 0)):
        sq_send[k] = normed_of(rel[k])
        if k:
            sq_copy(k).start()
        for c in range(chunks):
            cut = slice(c * cw, (c + 1) * cw)
            term = product(c)
            if t is not None:
                a_send[t * chunks + c] = term.astype(BF16)
                a_copy(t, c).start()
            elif k == 2:
                a_copy(0, c).wait_recv()
                b_send[c] = (term + a_recv[c].astype(F32)).astype(BF16)
                b_copy(c).start()
            else:
                own_v[:, cut] = term
    for k in (1, 2, 3):
        sq_copy(k).wait_recv()
    squares = sq_send[0] + sq_recv[1] + sq_recv[2] + sq_recv[3]
    squares = jnp.broadcast_to(squares[:1], (128, blk)).T[:, :1]
    inverse = lax.rsqrt(squares / (width * groups) + norm_eps)
    for c in range(chunks):
        cut = slice(c * cw, (c + 1) * cw)
        a_copy(1, c).wait_recv()
        b_copy(c).wait_recv()
        total = own_v[:, cut] + a_recv[chunks + c].astype(F32) + b_recv[c].astype(F32)
        out_ref[:, cut] = (total * inverse).astype(BF16)
    for copy in bc_copies:
        copy.wait_send()
    for k in range(1, reach + 1):

        @pl.when(sq + k < n_seq)
        def _():
            to_later(k).wait_send()

    for k in (1, 2, 3):
        sq_copy(k).wait_send()
    for c in range(chunks):
        a_copy(0, c).wait_send()
        a_copy(1, c).wait_send()
        b_copy(c).wait_send()


def on_device(
    x_in, z_gate, b_in, c_in, dt_raw, decay_rate, skip_gain, norm_gain, w_out, doc_lengths
):
    rows, width = x_in.shape
    heads = dt_raw.shape[1]
    head_size = width // heads
    groups, n_seq = lax.axis_size("head"), lax.axis_size("seq")
    blk = rows // groups
    longest = rows * n_seq // 4
    reach = min(-(-(longest - 1) // rows), n_seq - 1)
    d_model = w_out.shape[1]
    chunks = 5
    part = b_in.shape[1]
    n_state = part * groups
    bc = jnp.concatenate([b_in.T, c_in.T], axis=0)
    ends = jnp.cumsum(doc_lengths)
    skip = jnp.repeat(skip_gain, head_size)[None, :]
    cw = d_model // chunks
    vm = pl.BlockSpec(memory_space=pltpu.VMEM)
    hbm = pl.BlockSpec(memory_space=pl.ANY)
    dma = pltpu.SemaphoreType.DMA
    return pl.pallas_call(
        functools.partial(kernel, (n_seq, groups, blk, heads, reach, chunks)),
        out_shape=jax.ShapeDtypeStruct((blk, d_model), BF16),
        in_specs=[vm] * 5 + [pl.BlockSpec(memory_space=pltpu.SMEM)] + [hbm] * 3,
        out_specs=vm,
        scratch_shapes=[
            pltpu.VMEM((rows, width), BF16),
            pltpu.VMEM((rows, width), BF16),
            pltpu.VMEM(w_out.shape, BF16),
            pltpu.VMEM((groups, 2 * part, rows), BF16),
            pltpu.VMEM((groups, blk, width), BF16),
            pltpu.VMEM((groups, blk, 128), BF16),
            pltpu.VMEM((groups, n_state, width), BF16),
            pltpu.VMEM((groups, 8, width), F32),
            pltpu.VMEM((groups, blk, n_state), BF16),
            pltpu.VMEM((groups, blk, width), F32),
            pltpu.VMEM((groups, blk, width), F32),
            pltpu.VMEM((n_state + 16, width), BF16),
            pltpu.VMEM((reach, n_state + 16, width), BF16),
            pltpu.VMEM((n_state, width), F32),
            pltpu.VMEM((blk, width), BF16),
            pltpu.VMEM((blk, d_model), F32),
            pltpu.VMEM((2 * chunks, blk, cw), BF16),
            pltpu.VMEM((2 * chunks, blk, cw), BF16),
            pltpu.VMEM((chunks, blk, cw), BF16),
            pltpu.VMEM((chunks, blk, cw), BF16),
            pltpu.VMEM((4, 8, blk), F32),
            pltpu.VMEM((4, 8, blk), F32),
            dma((4,)),
            dma((4,)),
            dma((4,)),
            dma((reach,)),
            dma((reach,)),
            dma((4,)),
            dma((4,)),
            dma((2 * chunks,)),
            dma((2 * chunks,)),
            dma((chunks,)),
            dma((chunks,)),
        ],
        compiler_params=pltpu.CompilerParams(
            collective_id=0, has_side_effects=True, vmem_limit_bytes=60 * 1024 * 1024
        ),
        name="layer",
    )(bc, dt_raw.T, decay_rate[:, None], skip, norm_gain[None, :], ends, x_in, z_gate, w_out)


def solution(mesh):
    return jax.shard_map(
        on_device,
        mesh=mesh,
        in_specs=(
            P("seq", "head"),
            P("seq", "head"),
            P("seq", "head"),
            P("seq", "head"),
            P("seq", "head"),
            P("head"),
            P("head"),
            P("head"),
            P("head", None),
            P(),
        ),
        out_specs=P(("seq", "head"), None),
        check_vma=False,
    )
```

time: 183 us -> 69.7 us (0.38); the launches traced: 180 us -> 69.4 us
  Pallas kernels: 0 us -> 61.2 us
  waiting for transfers between devices: 48.1 us -> 0 us
  other arithmetic: 35.5 us -> 2.28 us
  blocking collectives: 32.1 us -> 0 us
  matrix products: 27.9 us -> 0 us
  local copies, waits for them, and re-layouts: 22.6 us -> 5.91 us
  between operations: 13.7 us -> 0.01 us
    pallas_call x0 -> x1, Pallas kernels: none -> 61.2 us  [on_device(): pl.pallas_call(functools.partial(kernel, (n_seq, groups, blk, heads, reac...]
    reduce_scatter x1 -> x0, waiting for transfers between devices: 41.6 us -> none  [on_device(): lax.psum_scatter(jnp.dot(normed, w_out, preferred_element_type=jnp.float3...]
    dot_general x6 -> x0, matrix products: 27.9 us -> none  [the longest x1 10.7 us: on_device(): jnp.dot(normed, w_out, preferred_element_type=jnp.float32)]
    all_gather x3 -> x0, blocking collectives: 26.4 us -> none  [the longest x1 14.5 us: entering(): lax.all_gather(part.astype(kind), axis)]
    reshape x4 -> x0, local copies, waits for them, and re-layouts: 11.5 us -> none  [the longest x1 5.5 us: on_device(): y_total.reshape(rows_here, local_width)]
    convert_element_type x14 -> x0, other arithmetic: 10.6 us -> none  [the longest x8 5.4 us: lap(): part[k].astype(own.dtype)]
    another operation x11 -> x2, other arithmetic: 9.88 us -> 0.75 us
    select_n x8 -> x0, other arithmetic: 8.7 us -> none  [lap(): return jax.tree.map(lambda a, b: jnp.where(reached, a, b), new, before)]
  transfers between devices with their start and end apart: 2 -> 0, of which waited for: 2 -> 0; matrix products, arithmetic and copies ran while one was open for 14% -> 0% of each run, Pallas kernels for 0% -> 0%
where the time goes in v1:
time: 69.7 us; the launch traced here: 69.4 us
  Pallas kernels  61.2 us (88%)
  local copies, waits for them, and re-layouts  5.91 us (8%)
  other arithmetic  2.28 us (3%)
    pallas_call x1, Pallas kernels, on_device(): pl.pallas_call(functools.partial(kernel, (n_seq, groups, blk, heads, reac...  61.2 us
    unnamed x1, local copies, waits for them, and re-layouts  2.46 us
    concatenate x1, other arithmetic, on_device(): bc = jnp.concatenate([b_in.T, c_in.T], axis=0)  1.53 us

profile of v1, /device:TPU:10, one launch (start us, length us, event | category | flops | bytes accessed | tf_op | source)
XLA Modules:
  0.0 69.4 jit_solution(17255306407908699106)
XLA Ops:
  0.0 1.3 %copy.14.rate_ref = f32[16,1]{1,0:T(8,128)} copy(f32[16,1]{0,1:T(1,128)} %bitcast.10) | data formatting | bytes 128 | tf_op jit(solution)/shard_map/broadcast_in_dim | solution.py:366
  1.3 0.7 %broadcast_in_dim.10 = f32[16,64]{1,0:T(8,128)S(1)} broadcast(f32[16]{0:T(128)} %param.16), dimensions={0} | broadcast | bytes 4160 | tf_op jit(solution)/shard_map/broadcast_in_dim | solution.py:317
  2.1 0.7 broadcast_in_dim_reshape.3.skip_ref
  2.7 0.7 %copy.13 = s32[32,1]{1,0:T(8,128)S(1)} copy(s32[32,1]{0,1:T(1,128)} %bitcast.11) | data formatting | bytes 256 | tf_op jit(solution)/shard_map/reshape.18
  3.5 0.1 reduce-window.9
  3.5 0.7 reduce.ends_ref
  4.2 1.5 %pad_maximum_fusion.bc_ref = bf16[64,1024]{1,0:T(8,128)(2,1)} fusion(bf16[32,1024]{1,0:T(8,128)(2,1)} %bitcast.7, bf16[32,1024]{1,0:T(8,128)(2,1)} %bitcast.8), kind=kLoop, calls=%fused_computation | loop fusion | flops 262144 | bytes 262144 | tf_op jit(solution)/shard_map/concatenate | solution.py:315
  5.7 61.2 %layer.1 = bf16[256,2560]{1,0:T(8,128)(2,1)} custom-call(bf16[64,1024]{1,0:T(8,128)(2,1)} %pad_maximum_fusion.bc_ref, f32[16,1024]{1,0:T(8,128)} %bitcast.6, f32[16,1]{1,0:T(8,128)} %copy.14.rate_ref, f32[1,1024]{1,0:T(1,128)} %broadcast_in_dim_reshape.3.skip_ref, f32[1,1024]{1,0:T(1,128)} %bitcast.9, s32[32]{0:T(128)} %reduce.ends_ref, ...), custom_call_target="tpu_custom_call" | custom-call | tf_op jit(solution)/shard_map/layer/pallas_call | solution.py:322
  67.0 2.5 %copy.16 = bf16[256,2560]{1,0:T(8,128)(2,1)} copy(bf16[256,2560]{1,0:T(8,128)(2,1)} %layer.1) | data formatting | bytes 2621440

commit v2 on v1

v2 whole, which is shorter than its diff:
```python
import functools

import jax
import jax.numpy as jnp
from jax import lax
from jax.experimental import pallas as pl
from jax.experimental.pallas import tpu as pltpu
from jax.sharding import PartitionSpec as P

norm_eps = 1e-05
MESH = pl.DeviceIdType.MESH
F32, BF16 = jnp.float32, jnp.bfloat16


def halves(v):
    high = v.astype(BF16).astype(F32)
    return high, v - high


def kernel(
    dims,
    b_ref,
    c_ref,
    dt_ref,
    gain_ref,
    rate_ref,
    skip_ref,
    lengths_ref,
    x_hbm,
    z_hbm,
    w_hbm,
    out_ref,
    x_v,
    z_v,
    w_v,
    turn_v,
    maps_v,
    xf_v,
    at_v,
    g_v,
    dec_v,
    cal_v,
    y_v,
    eg_v,
    st_send,
    st_recv,
    dc_send,
    dc_recv,
    gin_v,
    nrm_v,
    own_v,
    a_send,
    a_recv,
    b_send,
    b_recv,
    sq_send,
    sq_recv,
    loc_sem,
    mp_ssem,
    mp_rsem,
    st_ssem,
    st_rsem,
    sq_ssem,
    sq_rsem,
    a_ssem,
    a_rsem,
    b_ssem,
    b_rsem,
):
    n_seq, groups, blk, heads, reach, chunks = dims
    rows, width = x_v.shape
    part = b_ref.shape[1]
    n_state = part * groups
    head_size = width // heads
    cw = w_v.shape[1] // chunks
    hd = lax.axis_index("head")
    sq = lax.axis_index("seq")
    p1 = hd + 1 - 2 * (hd % 2)
    p2 = (hd + 2) % 4
    p3 = (p1 + 2) % 4
    rel = (hd, p1, p2, p3)

    loads = [
        pltpu.make_async_copy(src, dst, loc_sem.at[i])
        for i, (src, dst) in enumerate(
            ((x_hbm, x_v), (z_hbm, z_v), (w_hbm, w_v))
        )
    ]
    loads[0].start()

    barrier = pltpu.get_barrier_semaphore()
    for k in (1, 2, 3):
        pl.semaphore_signal(
            barrier, inc=1, device_id={"seq": sq, "head": rel[k]}, device_id_type=MESH
        )
    for k in range(1, reach + 1):
        for other in ((sq + k) % n_seq, (sq + n_seq - k) % n_seq):
            pl.semaphore_signal(
                barrier, inc=1, device_id={"seq": other, "head": hd}, device_id_type=MESH
            )
    turn_v[:, :part] = b_ref[...].astype(F32)
    turn_v[:, part : 2 * part] = c_ref[...].astype(F32)
    turn_v[:, 2 * part : 2 * part + heads] = dt_ref[...]
    turned = turn_v[...].T
    maps_v[0, 0] = turned[:part].astype(BF16)
    maps_v[1, 0] = turned[part : 2 * part].astype(BF16)
    dt_rows = turned[2 * part : 2 * part + heads]
    pl.semaphore_wait(barrier, 3 + 2 * reach)

    def to_head(k, src, dst, ssem, rsem):
        return pltpu.make_async_remote_copy(
            src_ref=src,
            dst_ref=dst,
            send_sem=ssem,
            recv_sem=rsem,
            device_id={"seq": sq, "head": rel[k]},
            device_id_type=MESH,
        )

    def map_copy(i, k):
        source = maps_v.at[i, 2 if k == 3 else 0]
        j = 4 * i + k
        return to_head(
            1 if k == 3 else k, source, maps_v.at[i, k], mp_ssem.at[j], mp_rsem.at[j]
        )

    for i in (0, 1):
        map_copy(i, 2).start()
        map_copy(i, 1).start()
    loads[1].start()
    loads[2].start()

    step = jnp.log(1.0 + jnp.exp(dt_rows))
    which = lax.broadcasted_iota(jnp.int32, (heads, 128), 0)
    lane_head = lax.broadcasted_iota(jnp.int32, (1, width), 1) // head_size
    rate = jnp.zeros((heads, 128), F32)
    skip = jnp.zeros((1, width), F32)
    for h in range(heads):
        rate = jnp.where(which == h, rate_ref[h], rate)
        skip = jnp.where(lane_head == h, skip_ref[h], skip)
    ld = -step * rate[:, :1]
    l1, rest = halves(ld)
    l2, l3 = halves(rest)
    split = jnp.concatenate([l1, l2, l3], axis=0).astype(BF16)
    ii = lax.broadcasted_iota(jnp.int32, (blk, blk), 0)
    jj = lax.broadcasted_iota(jnp.int32, (blk, blk), 1)
    upper = jnp.where(ii <= jj, 1.0, 0.0).astype(BF16)
    er = lax.broadcasted_iota(jnp.int32, (128, width), 0)
    ec = lax.broadcasted_iota(jnp.int32, (128, width), 1)
    lead = ec // head_size
    spread_f = jnp.where((er == lead) | (er == lead + heads), 1.0, 0.0).astype(BF16)
    spread_e = jnp.where(
        (er == lead + 2 * heads) | (er == lead + 3 * heads), 1.0, 0.0
    ).astype(BF16)
    pad = jnp.zeros((128 - 4 * heads, blk), F32)
    lasts, finals = [], []
    for s in range(groups):
        at = slice(s * blk, (s + 1) * blk)
        c3 = jnp.dot(split[:, at], upper, preferred_element_type=F32)
        cum = c3[:heads] + c3[heads : 2 * heads] + c3[2 * heads :]
        fh, fl = halves(jnp.exp(-cum) * step[:, at])
        grow = jnp.exp(cum)
        finals.append(jnp.broadcast_to(grow[:, blk - 1 :], (heads, 128)))
        eh, el = halves(grow)
        turned = jnp.concatenate([fh, fl, eh, el, pad], axis=0).T.astype(BF16)
        at_v[s] = turned
        lasts.append(
            jnp.dot(turned[blk - 16 :], spread_e, preferred_element_type=F32)[15:16]
        )
        if s == 0:
            loads[0].wait()
        fx = jnp.dot(turned, spread_f, preferred_element_type=F32)
        xf_v[s] = (x_v[at, :].astype(F32) * fx).astype(BF16)

    base = sq * rows
    pos = base + lax.broadcasted_iota(jnp.int32, (8, rows), 1)
    doc = jnp.zeros((8, rows), F32)
    marks = [base + s * blk - 1 for s in range(groups + 1)]
    tags = [jnp.float32(0.0)] * (groups + 1)
    end = 0
    for k in range(lengths_ref.shape[0]):
        end = end + lengths_ref[k]
        doc = doc + jnp.where(pos >= end, 1.0, 0.0)
        tags = [t + jnp.where(m >= end, 1.0, 0.0) for t, m in zip(tags, marks)]

    map_copy(0, 2).wait_recv()
    map_copy(0, 3).start()

    def later(j, k, source, place):
        i = 3 * (k - 1) + j
        return pltpu.make_async_remote_copy(
            src_ref=source,
            dst_ref=place.at[k - 1] if j == 2 else place.at[k - 1, j],
            send_sem=st_ssem.at[i],
            recv_sem=st_rsem.at[i],
            device_id={"seq": (sq + k) % n_seq, "head": hd},
            device_id_type=MESH,
        )

    def to_later(j, k):
        if j == 2:
            return later(j, k, dc_send, dc_recv)
        return later(j, k, st_send.at[j], st_recv)

    def send_later(j):
        for k in range(1, reach + 1):

            @pl.when(sq + k < n_seq)
            def _():
                to_later(j, k).start()

    half = n_state // 2
    decay = jnp.ones((1, width), F32)
    whole = jnp.ones((heads, 128), F32)
    alives = []
    for s in range(groups):
        dec_v[s] = jnp.broadcast_to(decay, (8, width))
        alive = jnp.where(tags[s] == tags[s + 1], 1.0, 0.0)
        alives.append(alive)
        decay = decay * (lasts[s] * alive)
        whole = whole * (finals[s] * alive)
    dc_send[...] = whole.astype(BF16)
    send_later(2)
    for j in (0, 1):
        map_copy(0, 2 * j + 1).wait_recv()
        bt = jnp.concatenate([maps_v[0, 2 * j], maps_v[0, 2 * j + 1]], axis=0)
        state = jnp.zeros((half, width), F32)
        for s in range(groups):
            at = slice(s * blk, (s + 1) * blk)
            g_v[s, j * half : (j + 1) * half, :] = state.astype(BF16)
            kept = jnp.where(doc[:1, at] == tags[s + 1], 1.0, 0.0)
            bm = (bt[:, at].astype(F32) * kept).astype(BF16)
            grown = jnp.dot(bm, xf_v[s], preferred_element_type=F32)
            state = lasts[s] * (alives[s] * state + grown)
        st_send[j] = state.astype(BF16)
        send_later(j)
        if j == 0:
            map_copy(1, 2).wait_recv()
            map_copy(1, 3).start()
    map_copy(1, 1).wait_recv()
    map_copy(1, 3).wait_recv()
    bt = jnp.concatenate([maps_v[0, k] for k in range(groups)], axis=0)
    ct = jnp.concatenate([maps_v[1, k] for k in range(groups)], axis=0)

    loads[1].wait()
    for s in range(groups):
        at = slice(s * blk, (s + 1) * blk)
        c_s = ct[:, at].astype(F32).T
        scores = jnp.dot(c_s.astype(BF16), bt[:, at], preferred_element_type=F32)
        row = doc[:1, at]
        col = jnp.broadcast_to(row, (128, blk)).T[:, :1]
        seen = (ii >= jj) & (col == row)
        scores = jnp.where(seen, scores, 0.0).astype(BF16)
        cal = (c_s * jnp.where(col == tags[s], 1.0, 0.0)).astype(BF16)
        cal_v[s] = cal
        ex = jnp.dot(at_v[s], spread_e, preferred_element_type=F32)
        y = jnp.dot(scores, xf_v[s], preferred_element_type=F32)
        y = y + jnp.dot(cal, g_v[s], preferred_element_type=F32)
        zf = z_v[at, :].astype(F32)
        gate = zf / (1.0 + jnp.exp(-zf))
        y_v[s] = (ex * y + skip * x_v[at, :].astype(F32)) * gate
        eg_v[s] = ex * gate

    loads[2].wait()
    for k in range(1, reach + 1):

        @pl.when(sq >= k)
        def _():
            for j in (2, 0, 1):
                to_later(j, k).wait_recv()

        @pl.when(sq < k)
        def _():
            st_recv[k - 1] = jnp.zeros(st_recv.shape[1:], BF16)
            dc_recv[k - 1] = jnp.zeros(dc_recv.shape[1:], BF16)

    fill = jnp.zeros((128 - heads, 128), F32)
    incoming = jnp.zeros((n_state, width), F32)
    for k in range(reach, 0, -1):
        came = st_recv[k - 1].reshape(n_state, width).astype(F32)
        if k < reach:
            turned = jnp.concatenate([dc_recv[k - 1].astype(F32), fill], axis=0).T[:16]
            times = jnp.dot(turned.astype(BF16), spread_f, preferred_element_type=F32)
            came = came + times[:1] * incoming
        incoming = came
    gin_v[...] = incoming

    def normed_of(q, slot):
        carried = (gin_v[...] * dec_v[q][:1]).astype(BF16)
        u = y_v[q] + eg_v[q] * jnp.dot(cal_v[q], carried, preferred_element_type=F32)
        total = jnp.sum(u * u, axis=1, keepdims=True)
        nrm_v[slot] = (u * gain_ref[...]).astype(BF16)
        return jnp.broadcast_to(total, (blk, 128)).T[:8]

    def product(c, slot):
        return jnp.dot(
            nrm_v[slot], w_v[:, c * cw : (c + 1) * cw], preferred_element_type=F32
        )

    def a_copy(t, c):
        i = t * chunks + c
        return to_head(1, a_send.at[i], a_recv.at[i], a_ssem.at[i], a_rsem.at[i])

    def b_copy(c):
        return to_head(2, b_send.at[c], b_recv.at[c], b_ssem.at[c], b_rsem.at[c])

    def sq_copy(k):
        return to_head(
            k, sq_send.at[k], sq_recv.at[k], sq_ssem.at[k], sq_rsem.at[k]
        )

    def give(t, c, slot):
        a_send[t * chunks + c] = product(c, slot).astype(BF16)
        a_copy(t, c).start()

    def pass_on(c):
        term = product(c, 1)
        a_copy(0, c).wait_recv()
        b_send[c] = (term + a_recv[c].astype(F32)).astype(BF16)
        b_copy(c).start()

    sums3 = normed_of(p3, 0)
    give(0, 0, 0)
    sums2 = normed_of(p2, 1)
    for c in range(chunks):
        if c + 1 < chunks:
            give(0, c + 1, 0)
        pass_on(c)
    sq_send[3] = sums3
    sq_send[2] = sums2
    sq_copy(3).start()
    sq_copy(2).start()
    sq_send[1] = normed_of(p1, 0)
    sq_copy(1).start()
    for c in range(chunks):
        give(1, c, 0)
    sq_send[0] = normed_of(hd, 1)
    for c in range(chunks):
        own_v[:, c * cw : (c + 1) * cw] = product(c, 1)
    for k in (1, 2, 3):
        sq_copy(k).wait_recv()
    squares = sq_send[0] + sq_recv[1] + sq_recv[2] + sq_recv[3]
    squares = jnp.broadcast_to(squares[:1], (128, blk)).T[:, :1]
    inverse = lax.rsqrt(squares / (width * groups) + norm_eps)
    for c in range(chunks):
        cut = slice(c * cw, (c + 1) * cw)
        a_copy(1, c).wait_recv()
        b_copy(c).wait_recv()
        total = own_v[:, cut] + a_recv[chunks + c].astype(F32) + b_recv[c].astype(F32)
        out_ref[:, cut] = (total * inverse).astype(BF16)
    for i in (0, 1):
        for k in (1, 2, 3):
            map_copy(i, k).wait_send()
    for k in range(1, reach + 1):

        @pl.when(sq + k < n_seq)
        def _():
            for j in (0, 1, 2):
                to_later(j, k).wait_send()

    for k in (1, 2, 3):
        sq_copy(k).wait_send()
    for c in range(chunks):
        a_copy(0, c).wait_send()
        a_copy(1, c).wait_send()
        b_copy(c).wait_send()


def on_device(
    x_in, z_gate, b_in, c_in, dt_raw, decay_rate, skip_gain, norm_gain, w_out, doc_lengths
):
    rows, width = x_in.shape
    heads = dt_raw.shape[1]
    head_size = width // heads
    groups, n_seq = lax.axis_size("head"), lax.axis_size("seq")
    blk = rows // groups
    longest = rows * n_seq // 4
    reach = min(-(-(longest - 1) // rows), n_seq - 1)
    d_model = w_out.shape[1]
    chunks = 5
    part = b_in.shape[1]
    n_state = part * groups
    cw = d_model // chunks
    vm = pl.BlockSpec(memory_space=pltpu.VMEM)
    hbm = pl.BlockSpec(memory_space=pl.ANY)
    dma = pltpu.SemaphoreType.DMA
    return pl.pallas_call(
        functools.partial(kernel, (n_seq, groups, blk, heads, reach, chunks)),
        out_shape=jax.ShapeDtypeStruct((blk, d_model), BF16),
        in_specs=[vm] * 4 + [pl.BlockSpec(memory_space=pltpu.SMEM)] * 3 + [hbm] * 3,
        out_specs=vm,
        scratch_shapes=[
            pltpu.VMEM((rows, width), BF16),
            pltpu.VMEM((rows, width), BF16),
            pltpu.VMEM(w_out.shape, BF16),
            pltpu.VMEM((rows, 128), F32),
            pltpu.VMEM((2, groups, part, rows), BF16),
            pltpu.VMEM((groups, blk, width), BF16),
            pltpu.VMEM((groups, blk, 128), BF16),
            pltpu.VMEM((groups, n_state, width), BF16),
            pltpu.VMEM((groups, 8, width), F32),
            pltpu.VMEM((groups, blk, n_state), BF16),
            pltpu.VMEM((groups, blk, width), F32),
            pltpu.VMEM((groups, blk, width), F32),
            pltpu.VMEM((2, n_state // 2, width), BF16),
            pltpu.VMEM((reach, 2, n_state // 2, width), BF16),
            pltpu.VMEM((heads, 128), BF16),
            pltpu.VMEM((reach, heads, 128), BF16),
            pltpu.VMEM((n_state, width), F32),
            pltpu.VMEM((2, blk, width), BF16),
            pltpu.VMEM((blk, d_model), F32),
            pltpu.VMEM((2 * chunks, blk, cw), BF16),
            pltpu.VMEM((2 * chunks, blk, cw), BF16),
            pltpu.VMEM((chunks, blk, cw), BF16),
            pltpu.VMEM((chunks, blk, cw), BF16),
            pltpu.VMEM((4, 8, blk), F32),
            pltpu.VMEM((4, 8, blk), F32),
            dma((3,)),
            dma((8,)),
            dma((8,)),
            dma((3 * reach,)),
            dma((3 * reach,)),
            dma((4,)),
            dma((4,)),
            dma((2 * chunks,)),
            dma((2 * chunks,)),
            dma((chunks,)),
            dma((chunks,)),
        ],
        compiler_params=pltpu.CompilerParams(
            collective_id=0, has_side_effects=True, vmem_limit_bytes=60 * 1024 * 1024
        ),
        name="layer",
    )(
        b_in,
        c_in,
        dt_raw,
        norm_gain[None, :],
        decay_rate,
        skip_gain,
        doc_lengths,
        x_in,
        z_gate,
        w_out,
    )


def solution(mesh):
    return jax.shard_map(
        on_device,
        mesh=mesh,
        in_specs=(
            P("seq", "head"),
            P("seq", "head"),
            P("seq", "head"),
            P("seq", "head"),
            P("seq", "head"),
            P("head"),
            P("head"),
            P("head"),
            P("head", None),
            P(),
        ),
        out_specs=P(("seq", "head"), None),
        check_vma=False,
    )
```

time: 69.7 us -> 63.4 us (0.910)
  Pallas kernels: 61.2 us -> 55.2 us
  other arithmetic: 2.28 us -> 0 us
  local copies, waits for them, and re-layouts: 5.91 us -> 7.67 us
    pallas_call x1, Pallas kernels: 61.2 us -> 55.2 us  [on_device(): pl.pallas_call(functools.partial(kernel, (n_seq, groups, blk, heads, reac...]
    unnamed x1 -> x4, local copies, waits for them, and re-layouts: 2.46 us -> 7.67 us
    broadcast_in_dim x2 -> x0, local copies, waits for them, and re-layouts: 2.05 us -> none  [the longest x1 1.33 us: on_device(): decay_rate[:, None]]
    concatenate x1 -> x0, other arithmetic: 1.53 us -> none  [on_device(): bc = jnp.concatenate([b_in.T, c_in.T], axis=0)]
    another operation x2 -> x0, local copies, waits for them, and re-layouts: 1.4 us -> none
    another operation x2 -> x0, other arithmetic: 0.75 us -> none
where the time goes in v2:
time: 63.4 us; the launch traced here: 62.9 us
  Pallas kernels  55.2 us (87%)
  local copies, waits for them, and re-layouts  7.67 us (12%)
    pallas_call x1, Pallas kernels, on_device(): pl.pallas_call(functools.partial(kernel, (n_seq, groups, blk, heads, reac...  55.2 us
    unnamed x4, local copies, waits for them, and re-layouts  7.67 us

profile of v2, /device:TPU:10, one launch (start us, length us, event | category | flops | bytes accessed | tf_op | source)
XLA Modules:
  0.0 62.9 jit_solution(7192899727648164813)
XLA Ops:
  0.0 1.7 %copy.11.b_ref = bf16[1024,32]{1,0:T(8,128)(2,1)} copy(bf16[1024,32]{0,1:T(8,128)(2,1)} %param.12) | data formatting | bytes 131072 | tf_op args[2]
  1.7 1.7 %copy.12.c_ref = bf16[1024,32]{1,0:T(8,128)(2,1)} copy(bf16[1024,32]{0,1:T(8,128)(2,1)} %param.13) | data formatting | bytes 131072 | tf_op args[3]
  3.4 1.8 %copy.13.dt_ref = f32[1024,16]{1,0:T(8,128)} copy(f32[1024,16]{0,1:T(8,128)} %param.14) | data formatting | bytes 131072 | tf_op args[4]
  5.2 55.2 %layer.1 = bf16[256,2560]{1,0:T(8,128)(2,1)} custom-call(bf16[1024,32]{1,0:T(8,128)(2,1)} %copy.11.b_ref, bf16[1024,32]{1,0:T(8,128)(2,1)} %copy.12.c_ref, f32[1024,16]{1,0:T(8,128)} %copy.13.dt_ref, f32[1,1024]{1,0:T(1,128)} %bitcast.1, f32[16]{0:T(128)} %rate_ref.1, f32[16]{0:T(128)} %skip_ref.1, s32[32]{0:T(128)} %lengths_ref.1, ...), custom_call_target="tpu_custom_call" | custom-call | tf_op jit(solution)/shard_map/layer/pallas_call | solution.py:387
  60.4 2.5 %copy.15 = bf16[256,2560]{1,0:T(8,128)(2,1)} copy(bf16[256,2560]{1,0:T(8,128)(2,1)} %layer.1) | data formatting | bytes 2621440
